TPU v7x, 128 devices: a whole 4x4x4 slice. The times are simulated.
128 devices in a mesh: replica: 1, data: 128 (over z, y, x, core).
Axes of the slice: x: 4, y: 4, z: 4, core: 2. Of those that a mesh axis runs over, the one named last changes fastest.
Arguments:
- query_hidden: bfloat16 [1024, 32, 768], P(('replica', 'data'))
- doc_hidden: bfloat16 [1024, 300, 768], P(('replica', 'data'))
- neg_hidden: bfloat16 [1024, 2, 300, 768], P(('replica', 'data'))
- query_mask: int32 [1024, 32], P(('replica', 'data'))
- doc_mask: int32 [1024, 300], P(('replica', 'data'))
- neg_mask: int32 [1024, 2, 300], P(('replica', 'data'))
- teacher: float32 [1024, 3], P(('replica', 'data'))
- w_proj: bfloat16 [768, 128], replicated
- temperature: float32 [], replicated
Outputs:
- output 1: float32 [1024], P(('replica', 'data'))
- output 2: float32 [1], P('replica')
All inputs are finite; a program needn't handle non-finite values.
Results may differ from a plain program's by a relative error of at most 0.001.
Values are sent between devices in bfloat16 or wider.
A program may use at most 1 GiB of HBM per device.

v0:
```python
import jax
import jax.numpy as jnp
from jax import lax
from jax.sharding import PartitionSpec as P


def project_tokens(hidden, w_proj):
    flat_hidden = hidden.reshape(-1, hidden.shape[-1])
    projected = jnp.dot(flat_hidden, w_proj, preferred_element_type=jnp.float32)
    projected = projected / jnp.sqrt(jnp.sum(projected * projected, axis=-1, keepdims=True))
    return projected.astype(jnp.bfloat16).reshape(hidden.shape[:-1] + (w_proj.shape[1],))


def hard_scores_of(query_tok, neg_tok, neg_mask):
    sim_tile = jnp.einsum('itd,iksd->itks', query_tok, neg_tok, preferred_element_type=jnp.float32)
    return jnp.sum(jnp.max(jnp.where(neg_mask[:, None] > 0, sim_tile, -jnp.inf), axis=3), axis=1)


def finish_loss(score_rows, positive, hard_scores, teacher, value_a11):
    logits = score_rows / value_a11
    pos_logit = positive / value_a11
    cross_ent = jax.nn.logsumexp(logits, axis=1) - pos_logit
    student = jnp.concatenate([pos_logit[:, None], hard_scores / value_a11], axis=1)
    student_log = jax.nn.log_softmax(student, axis=1)
    teacher_log = jax.nn.log_softmax(teacher, axis=1)
    return cross_ent + jnp.sum(jnp.exp(teacher_log) * (teacher_log - student_log), axis=1)


def solution(mesh):
    group_size = mesh.shape['data']
    batch_axes = ('replica', 'data')

    def local_loss(query_hidden, doc_hidden, neg_hidden, query_mask, doc_mask, neg_mask, teacher, w_proj, value_a11):
        local_batch = query_hidden.shape[0]
        query_tok = project_tokens(query_hidden, w_proj) * query_mask[:, :, None].astype(jnp.bfloat16)
        doc_tok = project_tokens(doc_hidden, w_proj)
        neg_tok = project_tokens(neg_hidden, w_proj)
        doc_valid = (doc_mask > 0)[None]
        query_steps = lax.all_gather(jnp.transpose(query_tok, (1, 0, 2)), 'data', axis=1, tiled=True)

        def token_step(running, query_step):
            sim_tile = jnp.einsum('id,jsd->ijs', query_step, doc_tok, preferred_element_type=jnp.float32)
            return running + jnp.max(jnp.where(doc_valid, sim_tile, -jnp.inf), axis=2), None

        start_cols = jnp.zeros((query_steps.shape[1], local_batch), jnp.float32)
        columns = lax.scan(token_step, start_cols, query_steps)[0]
        score_rows = lax.all_to_all(columns, 'data', 0, 1, tiled=True)
        my_index = lax.axis_index('data')
        own_block = lax.dynamic_slice_in_dim(score_rows, my_index * local_batch, local_batch, axis=1)
        hard_scores = hard_scores_of(query_tok, neg_tok, neg_mask)
        loss_rows = finish_loss(score_rows, jnp.diagonal(own_block), hard_scores, teacher, value_a11)
        loss_mean = lax.psum(jnp.sum(loss_rows), 'data') / (local_batch * group_size)
        return loss_rows, loss_mean.reshape(1)

    in_specs = (P(batch_axes, None, None), P(batch_axes, None, None), P(batch_axes, None, None, None),
                P(batch_axes, None), P(batch_axes, None), P(batch_axes, None, None), P(batch_axes, None),
                P(None, None), P())
    out_specs = (P(batch_axes), P('replica'))
    return jax.shard_map(local_loss, mesh=mesh, in_specs=in_specs, out_specs=out_specs, check_vma=False)
```

profile of v0, /device:TPU:1, one launch (start us, length us, event | category | flops | bytes accessed | tf_op | source)
XLA Modules:
  0.0 275.1 jit_solution(833302199632300046)
XLA Ops:
  7.2 0.9 copy-done
  8.2 1.2 multiply_reduce_fusion.2
  11.9 7.1 %copy.33 = bf16[8,2,300,768]{3,2,1,0:T(8,128)(2,1)} copy(bf16[8,2,300,768]{3,1,2,0:T(2,128)(2,1)} %param.14) | data formatting | bytes 14745600 | tf_op args[2]
  19.0 8.9 %reshape.71 = bf16[4800,768]{1,0:T(8,128)(2,1)} reshape(bf16[8,2,300,768]{3,2,1,0:T(8,128)(2,1)} %copy.33) | data formatting | bytes 14745600 | tf_op jit(solution)/shard_map/reshape | solution.py:8
  27.8 5.3 %multiply_reduce_fusion = (f32[4800]{0:T(1024)S(1)}, f32[4800,128]{1,0:T(8,128)S(1)}) fusion(bf16[4800,768]{1,0:T(8,128)(2,1)} %reshape.71, bf16[768,128]{1,0:T(8,128)(2,1)S(1)} %copy-done.1), kind=kOutput, calls=%fused_computation.7 | convolution fusion | flops 944942400 | bytes 10046208 | tf_op jit(solution)/shard_map/dot_general | solution.py:9
  33.2 2.1 divide_convert_fusion
  36.2 4.6 %copy.29 = bf16[8,300,768]{2,1,0:T(8,128)(2,1)} copy(bf16[8,300,768]{2,0,1:T(8,128)(2,1)} %param.13) | data formatting | bytes 7372800 | tf_op args[1]
  40.8 4.7 %reshape.69 = bf16[2400,768]{1,0:T(8,128)(2,1)} reshape(bf16[8,300,768]{2,1,0:T(8,128)(2,1)} %copy.29) | data formatting | bytes 7372800 | tf_op jit(solution)/shard_map/reshape | solution.py:8
  45.5 3.3 %multiply_reduce_fusion.1 = (f32[2400]{0:T(1024)S(1)}, f32[2400,128]{1,0:T(8,128)S(1)}) fusion(bf16[2400,768]{1,0:T(8,128)(2,1)} %reshape.69, bf16[768,128]{1,0:T(8,128)(2,1)S(1)} %copy-done.1), kind=kOutput, calls=%fused_computation.10 | convolution fusion | flops 472471200 | bytes 5121408 | tf_op jit(solution)/shard_map/dot_general | solution.py:9
  50.5 42.1 %all-gather.2.cloned.1.call-done = bf16[32,1024,128]{2,1,0:T(8,128)(2,1)} async-done(((bf16[32,8,128]{2,1,0:T(8,128)(2,1)}), bf16[32,1024,128]{2,1,0:T(8,128)(2,1)}) %all-gather.2.cloned.1.call-update) | async-done | bytes 8388624 | tf_op jit(solution)/shard_map/all_gather | solution.py:39
  92.7 85.9 %while.11 = (s32[]{:T(128)}, f32[1024,8]{0,1:T(8,128)S(1)}, pred[1,8,300]{2,1,0:T(8,128)(4,1)S(1)}, bf16[32,1024,128]{2,1,0:T(8,128)(2,1)}, bf16[8,300,128]{2,1,0:T(8,128)(2,1)S(1)}, /*index=5*/s32[]{:T(128)}, s32[]{:T(128)}) while((s32[]{:T(128)}, f32[1024,8]{0,1:T(8,128)S(1)}, pred[1,8,300]{2,1,0:T(8,128)(4,1)S(1)}, ...), condition=%wide.region_4.5_spmd.clone, body=%wide.region_2.4_spmd.clone.sunk | while | flops 634068992 | bytes 1010115 | solution.py:46
  92.7 2.6 select_reduce_fusion.2
  95.3 2.6 select_reduce_fusion.2
  98.0 2.6 select_reduce_fusion.2
  100.7 2.6 select_reduce_fusion.2
  103.4 2.6 select_reduce_fusion.2
  106.1 2.6 select_reduce_fusion.2
  108.8 2.6 select_reduce_fusion.2
  111.4 2.6 select_reduce_fusion.2
  114.1 2.6 select_reduce_fusion.2
  116.8 2.6 select_reduce_fusion.2
  119.5 2.6 select_reduce_fusion.2
  122.2 2.6 select_reduce_fusion.2
  124.9 2.6 select_reduce_fusion.2
  127.6 2.6 select_reduce_fusion.2
  130.2 2.6 select_reduce_fusion.2
  132.9 2.6 select_reduce_fusion.2
  135.6 2.6 select_reduce_fusion.2
  138.3 2.6 select_reduce_fusion.2
  141.0 2.6 select_reduce_fusion.2
  143.7 2.6 select_reduce_fusion.2
  146.4 2.6 select_reduce_fusion.2
  149.1 2.6 select_reduce_fusion.2
  151.7 2.6 select_reduce_fusion.2
  154.4 2.6 select_reduce_fusion.2
  157.1 2.6 select_reduce_fusion.2
  159.8 2.6 select_reduce_fusion.2
  162.5 2.6 select_reduce_fusion.2
  165.2 2.6 select_reduce_fusion.2
  167.9 2.6 select_reduce_fusion.2
  170.5 2.6 select_reduce_fusion.2
  173.2 2.6 select_reduce_fusion.2
  175.9 2.6 select_reduce_fusion.2
  178.9 1.1 copy.30
  180.0 7.5 %all-to-all-start = ((f32[128,8,8]{1,2,0:T(8,128)}), f32[128,8,8]{1,2,0:T(8,128)S(1)}, u32[]{:S(2)}, u32[]{:S(2)}) async-start(f32[128,8,8]{1,2,0:T(8,128)} %copy.30), calls=%async_computation | async-start | bytes 1048576 | tf_op jit(solution)/shard_map/all_to_all | solution.py:47
  187.5 13.4 %all-to-all-done = f32[128,8,8]{1,2,0:T(8,128)S(1)} async-done(((f32[128,8,8]{1,2,0:T(8,128)}), f32[128,8,8]{1,2,0:T(8,128)S(1)}, u32[]{:S(2)}, u32[]{:S(2)}) %all-to-all-start) | async-done | bytes 32800 | tf_op jit(solution)/shard_map/all_to_all | solution.py:47
  202.6 1.1 fusion.11
  203.8 62.8 %psum.7 = f32[]{:T(128)} all-reduce(f32[]{:T(128)} %get-tuple-element.59), channel_id=1, replica_groups=mesh['replica'=1,'data'=128] {'data'}, use_global_device_ids=true, to_apply=%region_14.16 | all-reduce | flops 1 | bytes 8 | tf_op jit(solution)/shard_map/psum | solution.py:52
  (77 shorter events, 6.7 us)
Async XLA Ops:
  7.2 1.0 copy-start
  7.2 85.5 %all-gather.2.cloned.1.call-start = ((), (), s32[]{:S(2)}) async-start(), calls=%async_computation.1 | async-start | bytes 8454144 | tf_op jit(solution)/shard_map/all_gather | solution.py:39
  19.0 8.9 %copy-start.1 = (bf16[768,128]{1,0:T(8,128)(2,1)S(1)}, bf16[768,128]{1,0:T(8,128)(2,1)}, u32[]{:S(2)}) copy-start(bf16[768,128]{1,0:T(8,128)(2,1)} %param.19) | copy-start | bytes 589828
  48.8 0.7 copy-start.4
  48.8 0.7 copy-start.2
  48.8 1.7 copy-start.3
  180.0 20.9 %all-to-all-start = ((f32[128,8,8]{1,2,0:T(8,128)}), f32[128,8,8]{1,2,0:T(8,128)S(1)}, u32[]{:S(2)}, u32[]{:S(2)}) async-start(f32[128,8,8]{1,2,0:T(8,128)} %copy.30), calls=%async_computation | async-start | bytes 1048576 | tf_op jit(solution)/shard_map/all_to_all | solution.py:47
Sparse Core Ops, SparseCore 0:
  11.2 81.4 all-gather.1
where the time goes:
time: 277 us; the launch traced here: 275 us
  matrix products  95.1 us (34%)
  blocking collectives  62.8 us (23%)
  waiting for transfers between devices  55.5 us (20%)
  local copies, waits for them, and re-layouts  29.9 us (11%)
  between operations  16.6 us (6%)
  starting transfers between devices  7.52 us (3%)
  other arithmetic  6.63 us (2%)
    dot_general x32, matrix products, token_step(): jnp.einsum('id,jsd->ijs', query_step, doc_tok, preferred_element_type=jnp...  84.6 us
    psum x1, blocking collectives, local_loss(): lax.psum(jnp.sum(loss_rows), 'data') / (local_batch * group_size)  62.8 us
    all_gather x1, waiting for transfers between devices, local_loss(): lax.all_gather(jnp.transpose(query_tok, (1, 0, 2)), 'data', axis=1, tiled...  42.1 us
    unnamed x14, local copies, waits for them, and re-layouts  13.7 us
    reshape x2, local copies, waits for them, and re-layouts, project_tokens(): flat_hidden = hidden.reshape(-1, hidden.shape[-1])  13.6 us
    all_to_all x1, waiting for transfers between devices, local_loss(): score_rows = lax.all_to_all(columns, 'data', 0, 1, tiled=True)  13.4 us
    dot_general x3, matrix products, project_tokens(): projected = jnp.dot(flat_hidden, w_proj, preferred_element_type=jnp.float32)  9.82 us
    all_to_all x1, starting transfers between devices, local_loss(): score_rows = lax.all_to_all(columns, 'data', 0, 1, tiled=True)  7.48 us
  transfers between devices with their start and end apart: 2, of which 2 were waited for; matrix products, arithmetic and copies ran while one was open for 14% of the time, Pallas kernels for 0%

commit v1 on v0

v1 whole, which is shorter than its diff:
```python
import functools

import jax
import jax.numpy as jnp
from jax import lax
from jax.experimental import pallas as pl
from jax.experimental.pallas import tpu as pltpu
from jax.sharding import PartitionSpec as P

PAIRS, QLEN, DLEN, DPAD, HID, DIM = 8, 32, 300, 304, 768, 128
CHIPS, CORES, DEVICES = 64, 2, 128
LANES = PAIRS * QLEN
GROUPS, PER_GROUP = 8, 8


def hops(offset):
    return (0, 1, 2, 1)[offset]


def plan():
    tiles = [(dx, k1, k2) for dx in range(4) for k1 in range(4) for k2 in range(4)]
    gen = lambda t: (t[0] != 0) + hops(t[1]) + hops(t[2])
    dist = lambda t: sum(hops(o) for o in t)
    order = sorted(tiles, key=lambda t: (gen(t), dist(t), t))
    first, rest = order[:8], order[8:]
    waits = [[], rest[:16]] + [rest[16 + 8 * n:24 + 8 * n] for n in range(5)] + [[]]
    near = [t for t in rest if gen(t) == 2 and dist(t) == 2][:8]
    middle = [t for t in rest if t not in near]
    groups = [first] + [middle[8 * n:8 * n + 8] for n in range(6)] + [near]
    return first, waits, groups


def step_of(dx, axis, amount):
    along_y = (dx % 2 == 0) == (axis == 0)
    return (amount, 0) if along_y else (0, amount)


def forwards(tile):
    dx, k1, k2 = tile
    even = dx < 2
    go, back = (3, 1) if even else (1, -1)
    out = []
    if k1 == 0 and k2 == 0:
        out += [step_of(dx, 0, 1), step_of(dx, 0, -1)]
    if k2 == 0:
        out += [step_of(dx, 1, 1), step_of(dx, 1, -1)]
        if k1 == go:
            out.append(step_of(dx, 0, back))
    elif k2 == go:
        out.append(step_of(dx, 1, back))
    return out


def unit_rows(product):
    return product * lax.rsqrt(jnp.sum(product * product, axis=-1, keepdims=True))


def fold_lanes(row, shifts, combine):
    for shift in shifts:
        row = combine(row, pltpu.roll(row, shift, axis=1))
    return row


def kernel(qh_hbm, dh_hbm, nh_hbm, w_ref, qmask_ref, dmask_ref, nmask_ref, teacher_ref, tau_ref,
           loss_ref, mean_ref,
           qh, hidden, tiles, docs, negs, lens, hard, res_out, res_in, sum_out, sum_in,
           load_sem, q_sem, tile_send, tile_recv, doc_send, doc_recv, res_send, res_recv, sum_send, sum_recv):
    first, waits, groups = plan()
    me = lax.axis_index('data')
    core, chip = lax.rem(me, 2), lax.div(me, 2)
    cx, cy, cz = lax.rem(chip, 4), lax.rem(lax.div(chip, 4), 4), lax.div(chip, 16)
    wrap = lambda v: lax.rem(v + 8, 4)

    def chip_at(dx, dy, dz):
        return wrap(cz + dz) * 16 + wrap(cy + dy) * 4 + wrap(cx + dx)

    def target(dx, dy, dz):
        return {'data': chip_at(dx, dy, dz) * 2 + core}

    def slot_of(tile):
        dx, k1, k2 = tile
        return chip_at(dx, k1, k2) if dx % 2 == 0 else chip_at(dx, k2, k1)

    def tile_copy(slot, device):
        return pltpu.make_async_remote_copy(
            src_ref=tiles.at[slot], dst_ref=tiles.at[slot], send_sem=tile_send, recv_sem=tile_recv.at[slot],
            device_id=device, device_id_type=pl.DeviceIdType.MESH)

    def await_tile(tile):
        tile_copy(slot_of(tile), target(1, 0, 0)).wait_recv()

    def pass_on(tile):
        for dy, dz in forwards(tile):
            tile_copy(slot_of(tile), target(0, dy, dz)).start()

    load_q = pltpu.make_async_copy(qh_hbm, qh, q_sem)
    load_q.start()
    load_docs = [pltpu.make_async_copy(dh_hbm.at[j], hidden.at[j], load_sem.at[j]) for j in range(8)]
    load_negs = [pltpu.make_async_copy(nh_hbm.at[j // 2, j % 2], hidden.at[8 + j], load_sem.at[8 + j])
                 for j in range(16)]
    for copy in load_docs + load_negs:
        copy.start()

    barrier = pltpu.get_barrier_semaphore()
    for move in ((1, 0, 0), (2, 0, 0), (3, 0, 0), (0, 1, 0), (0, 3, 0), (0, 0, 1), (0, 0, 3)):
        pl.semaphore_signal(barrier, inc=1, device_id=target(*move), device_id_type=pl.DeviceIdType.MESH)
    pl.semaphore_signal(barrier, inc=1, device_id={'data': chip * 2 + 1 - core}, device_id_type=pl.DeviceIdType.MESH)

    w = w_ref[...]
    lane = lax.broadcasted_iota(jnp.int32, (1, LANES), 1)

    load_q.wait()
    q_unit = unit_rows(jnp.dot(qh[...].reshape(LANES, HID), w, preferred_element_type=jnp.float32)).astype(jnp.bfloat16)
    row_id = lax.broadcasted_iota(jnp.int32, (LANES, LANES), 0)
    col_id = lax.broadcasted_iota(jnp.int32, (LANES, LANES), 1)
    shuffle = (row_id == (col_id & 7) * QLEN + (col_id >> 3)).astype(jnp.float32).astype(jnp.bfloat16)
    q_cols = lax.dot_general(q_unit, shuffle, (((0,), (0,)), ((), ())), preferred_element_type=jnp.float32)
    q_len = jnp.sum(qmask_ref[...].astype(jnp.float32), axis=1, keepdims=True)
    sub8 = lax.broadcasted_iota(jnp.int32, (PAIRS, LANES), 0)
    lane8 = lax.broadcasted_iota(jnp.int32, (PAIRS, LANES), 1)
    q_live = jnp.where(((lane8 >> 3).astype(jnp.float32) < q_len) & ((lane8 & 7) == sub8), 1.0, 0.0)
    q_live = jnp.sum(q_live, axis=0, keepdims=True)
    tiles[chip] = jnp.where(q_live > 0, q_cols, 0.0).astype(jnp.bfloat16)

    d_len = jnp.sum(dmask_ref[...], axis=1, keepdims=True)
    lens[pl.ds(0, 8)] = jnp.broadcast_to(d_len, (8, 128))
    n_len = jnp.sum(nmask_ref[...], axis=2, keepdims=True)
    for j in range(16):
        lens[pl.ds(8 + j, 1)] = jnp.broadcast_to(n_len[j // 2, j % 2:j % 2 + 1], (1, 128))

    pl.semaphore_wait(barrier, 8)
    for dx in (1, 3, 2):
        tile_copy(chip, target(dx, 0, 0)).start()
    pass_on((0, 0, 0))

    row304 = lax.broadcasted_iota(jnp.int32, (DPAD, DIM), 0)

    def project(j):
        unit = unit_rows(jnp.dot(hidden[j], w, preferred_element_type=jnp.float32))
        unit = jnp.concatenate([unit, unit[:DPAD - DLEN]], axis=0)
        return jnp.where(row304 < lens[pl.ds(j, 1)], unit, unit[0:1]).astype(jnp.bfloat16)

    for copy in load_docs:
        copy.wait()
    for j in range(8):
        docs[core, j] = project(j)

    for copy in load_negs:
        copy.wait()
    doc_copy = pltpu.make_async_remote_copy(
        src_ref=docs.at[core], dst_ref=docs.at[core], send_sem=doc_send, recv_sem=doc_recv,
        device_id={'data': chip * 2 + 1 - core}, device_id_type=pl.DeviceIdType.MESH)
    doc_copy.start()

    def neg_body(n, carry):
        for u in range(8):
            negs[n * 8 + u] = project(8 + n * 8 + u)
        return carry

    lax.fori_loop(0, 2, neg_body, 0)

    for tile in first[1:]:
        await_tile(tile)
        pass_on(tile)

    def best(doc_at, cols):
        rows = []
        for j in range(16):
            sim = jnp.dot(doc_at(j), cols, preferred_element_type=jnp.float32)
            rows.append(jnp.max(sim, axis=0, keepdims=True))
        best_rows = jnp.concatenate(rows, axis=0)
        return fold_lanes(best_rows[:, :128] + best_rows[:, 128:], (8, 16, 32, 64), jnp.add)

    hard[...] = best(lambda j: negs[j], tiles[chip])
    doc_copy.wait_recv()

    sub16 = lax.broadcasted_iota(jnp.int32, (16, 128), 0)
    lane16 = lax.broadcasted_iota(jnp.int32, (16, 128), 1)
    keep = (lane16 >> 3) == sub16

    def score(slot):
        block = best(lambda j: docs[j // 8, j % 8], tiles[slot])
        res_out[slot] = jnp.sum(jnp.where(keep, block, 0.0), axis=0, keepdims=True)

    def slot_in_group(g, u):
        codes = []
        for tile in (group[u] for group in groups):
            dx, k1, k2 = tile
            dy, dz = (k1, k2) if dx % 2 == 0 else (k2, k1)
            codes.append(dz * 16 + dy * 4 + dx)
        code = codes[0]
        for n in range(1, GROUPS):
            code = jnp.where(g == n, codes[n], code)
        return chip_at(lax.rem(code, 4), lax.rem(lax.div(code, 4), 4), lax.div(code, 16))

    def res_copy(slot):
        return pltpu.make_async_remote_copy(
            src_ref=res_out.at[slot], dst_ref=res_in.at[chip], send_sem=res_send, recv_sem=res_recv,
            device_id={'data': slot * 2 + core}, device_id_type=pl.DeviceIdType.MESH)

    def send_results(g):
        for u in range(PER_GROUP):
            slot = slot_in_group(g, u)

            @pl.when(slot != chip)
            def _():
                res_copy(slot).start()

    def group_body(g, carry):
        for n in range(1, GROUPS):
            if waits[n]:
                @pl.when(g == n)
                def _(n=n):
                    for tile in waits[n]:
                        await_tile(tile)
                        pass_on(tile)

        @pl.when(g > 0)
        def _():
            send_results(g - 1)

        for u in range(PER_GROUP):
            score(slot_in_group(g, u))
        return carry

    lax.fori_loop(0, GROUPS, group_body, 0)
    send_results(GROUPS - 1)

    tau = tau_ref[0, 0]
    fold8 = (8, 16, 32, 64)
    sub = lax.broadcasted_iota(jnp.int32, (8, 128), 0)
    col = lax.broadcasted_iota(jnp.int32, (8, 128), 1)
    row_lane = lax.broadcasted_iota(jnp.int32, (1, 128), 1)
    own = res_out[chip]
    res_in[chip] = own
    pos = fold_lanes(jnp.where((row_lane >> 3) == core * 8 + (row_lane & 7), own, 0.0), fold8, jnp.add) / tau
    hard_all = hard[...]
    student = [pos] + [jnp.sum(jnp.where(sub16 == 2 * (lane16 & 7) + k, hard_all, 0.0), axis=0, keepdims=True) / tau
                       for k in range(2)]
    teacher = [jnp.sum(jnp.where((col & 7) == sub, jnp.broadcast_to(teacher_ref[:, k:k + 1], (8, 128)), 0.0),
                       axis=0, keepdims=True) for k in range(3)]

    def log_softmax(rows):
        top = jnp.maximum(jnp.maximum(rows[0], rows[1]), rows[2])
        total = jnp.exp(rows[0] - top) + jnp.exp(rows[1] - top) + jnp.exp(rows[2] - top)
        return [row - top - jnp.log(total) for row in rows]

    student_log, teacher_log = log_softmax(student), log_softmax(teacher)
    kl = sum(jnp.exp(t) * (t - s) for s, t in zip(student_log, teacher_log))

    pltpu.make_async_remote_copy(
        src_ref=res_out.at[pl.ds(0, CHIPS - 1)], dst_ref=res_in.at[pl.ds(0, CHIPS - 1)], send_sem=res_send,
        recv_sem=res_recv, device_id=target(1, 0, 0), device_id_type=pl.DeviceIdType.MESH).wait_recv()
    logits = res_in[...] / tau
    top = fold_lanes(jnp.max(logits, axis=0), fold8, jnp.maximum)
    total = fold_lanes(jnp.sum(jnp.exp(logits - top), axis=0), fold8, jnp.add)
    loss = top + jnp.log(total) - pos + kl
    loss_ref[...] = loss[:, :PAIRS]

    part = fold_lanes(loss, (1, 2, 4), jnp.add)
    sum_out[...] = part
    sum_in[me] = part

    def sum_copy(n):
        return pltpu.make_async_remote_copy(
            src_ref=sum_out, dst_ref=sum_in.at[me], send_sem=sum_send, recv_sem=sum_recv,
            device_id={'data': lax.rem(me + n, DEVICES)}, device_id_type=pl.DeviceIdType.MESH)

    def send_sum(n, carry):
        sum_copy(n).start()
        return carry

    lax.fori_loop(1, DEVICES, send_sum, 0)

    doc_copy.wait_send()
    pltpu.make_async_remote_copy(
        src_ref=tiles.at[pl.ds(0, CHIPS - 1)], dst_ref=tiles.at[pl.ds(0, CHIPS - 1)], send_sem=tile_send,
        recv_sem=tile_recv.at[0], device_id=target(1, 0, 0), device_id_type=pl.DeviceIdType.MESH).wait_send()
    pltpu.make_async_remote_copy(
        src_ref=res_out.at[pl.ds(0, CHIPS - 1)], dst_ref=res_in.at[pl.ds(0, CHIPS - 1)], send_sem=res_send,
        recv_sem=res_recv, device_id=target(1, 0, 0), device_id_type=pl.DeviceIdType.MESH).wait_send()
    all_sums = pltpu.make_async_remote_copy(
        src_ref=sum_in.at[pl.ds(0, DEVICES - 1)], dst_ref=sum_in.at[pl.ds(0, DEVICES - 1)], send_sem=sum_send,
        recv_sem=sum_recv, device_id=target(1, 0, 0), device_id_type=pl.DeviceIdType.MESH)
    all_sums.wait_recv()
    mean_ref[...] = (jnp.sum(sum_in[...], axis=0) / (PAIRS * DEVICES))[:, :1]
    all_sums.wait_send()


def solution(mesh):
    batch = ('replica', 'data')

    def local_loss(query_hidden, doc_hidden, neg_hidden, query_mask, doc_mask, neg_mask, teacher, w_proj, temperature):
        vmem, anyspace = pl.BlockSpec(memory_space=pltpu.VMEM), pl.BlockSpec(memory_space=pl.ANY)
        dma = pltpu.SemaphoreType.DMA
        loss, mean = pl.pallas_call(
            kernel,
            name='late_interaction',
            out_shape=(jax.ShapeDtypeStruct((1, PAIRS), jnp.float32), jax.ShapeDtypeStruct((1, 1), jnp.float32)),
            in_specs=[anyspace] * 3 + [vmem] * 5 + [pl.BlockSpec(memory_space=pltpu.SMEM)],
            out_specs=(vmem, vmem),
            scratch_shapes=[
                pltpu.VMEM((PAIRS, QLEN, HID), jnp.bfloat16),
                pltpu.VMEM((24, DLEN, HID), jnp.bfloat16),
                pltpu.VMEM((CHIPS, DIM, LANES), jnp.bfloat16),
                pltpu.VMEM((CORES, 8, DPAD, DIM), jnp.bfloat16),
                pltpu.VMEM((16, DPAD, DIM), jnp.bfloat16),
                pltpu.VMEM((24, 128), jnp.int32),
                pltpu.VMEM((16, 128), jnp.float32),
                pltpu.VMEM((CHIPS, 1, 128), jnp.float32),
                pltpu.VMEM((CHIPS, 1, 128), jnp.float32),
                pltpu.VMEM((1, 128), jnp.float32),
                pltpu.VMEM((DEVICES, 1, 128), jnp.float32),
                dma((24,)), dma, dma, dma((CHIPS,)), dma, dma, dma, dma, dma, dma,
            ],
            compiler_params=pltpu.CompilerParams(
                collective_id=0, has_side_effects=True, vmem_limit_bytes=60 * 2**20),
        )(query_hidden, doc_hidden, neg_hidden, w_proj, query_mask, doc_mask, neg_mask, teacher,
          temperature.reshape(1, 1))
        return loss.reshape(PAIRS), mean.reshape(1)

    in_specs = (P(batch, None, None), P(batch, None, None), P(batch, None, None, None), P(batch, None), P(batch, None),
                P(batch, None, None), P(batch, None), P(None, None), P())
    return jax.shard_map(local_loss, mesh=mesh, in_specs=in_specs, out_specs=(P(batch), P('replica')), check_vma=False)
```

time: 277 us -> 98.3 us (0.35)
  matrix products: 95.1 us -> 0 us
  Pallas kernels: 0 us -> 83.7 us
  blocking collectives: 62.8 us -> 0 us
  waiting for transfers between devices: 55.5 us -> 0 us
  local copies, waits for them, and re-layouts: 29.9 us -> 11.4 us
  between operations: 16.6 us -> 3.02 us
  starting transfers between devices: 7.52 us -> 0 us
  other arithmetic: 6.63 us -> 0 us
    dot_general x36 -> x0, matrix products: 95.1 us -> none  [the longest x32 84.6 us: token_step(): jnp.einsum('id,jsd->ijs', query_step, doc_tok, preferred_element_type=jnp...]
    pallas_call x0 -> x1, Pallas kernels: none -> 83.7 us  [local_loss(): pl.pallas_call(kernel, name='late_interaction', out_shape=(jax.ShapeDtype...]
    psum x1 -> x0, blocking collectives: 62.8 us -> none  [local_loss(): lax.psum(jnp.sum(loss_rows), 'data') / (local_batch * group_size)]
    all_gather x1 -> x0, waiting for transfers between devices: 42.1 us -> none  [local_loss(): lax.all_gather(jnp.transpose(query_tok, (1, 0, 2)), 'data', axis=1, tiled...]
    reshape x4 -> x0, local copies, waits for them, and re-layouts: 13.9 us -> none  [the longest x2 13.6 us: project_tokens(): flat_hidden = hidden.reshape(-1, hidden.shape[-1])]
    all_to_all x1 -> x0, waiting for transfers between devices: 13.4 us -> none  [local_loss(): score_rows = lax.all_to_all(columns, 'data', 0, 1, tiled=True)]
    all_to_all x1 -> x0, starting transfers between devices: 7.48 us -> none  [local_loss(): score_rows = lax.all_to_all(columns, 'data', 0, 1, tiled=True)]
    convert_element_type x4 -> x0, other arithmetic: 3.28 us -> none  [the longest x3 2.58 us: project_tokens(): projected.astype(jnp.bfloat16)]
  transfers between devices with their start and end apart: 2 -> 0, of which waited for: 2 -> 0; matrix products, arithmetic and copies ran while one was open for 14% -> 0% of each run, Pallas kernels for 0% -> 0%
where the time goes in v1:
time: 98.3 us; the launch traced here: 98.1 us
  Pallas kernels  83.7 us (85%)
  local copies, waits for them, and re-layouts  11.4 us (12%)
  between operations  3.02 us (3%)
    pallas_call x1, Pallas kernels, local_loss(): pl.pallas_call(kernel, name='late_interaction', out_shape=(jax.ShapeDtype...  83.7 us
    unnamed x6, local copies, waits for them, and re-layouts  11.4 us

profile of v1, /device:TPU:1, one launch (start us, length us, event | category | flops | bytes accessed | tf_op | source)
XLA Modules:
  0.0 98.1 jit_solution(16657439776120916650)
XLA Ops:
  1.3 1.3 %copy.13.teacher_ref = f32[8,3]{1,0:T(8,128)} copy(f32[8,3]{0,1:T(4,128)} %param.15) | data formatting | bytes 192 | tf_op args[6]
  2.6 0.0 copy-start
  2.6 4.8 %copy.11.dh_hbm = bf16[8,300,768]{2,1,0:T(8,128)(2,1)} copy(bf16[8,300,768]{2,0,1:T(8,128)(2,1)} %param.10) | data formatting | bytes 7372800 | tf_op args[1]
  7.5 0.1 copy-done
  7.5 4.0 %copy.12.nh_hbm = bf16[8,2,300,768]{3,2,1,0:T(8,128)(2,1)} copy(bf16[8,2,300,768]{3,1,2,0:T(2,128)(2,1)S(1)} %copy-done) | data formatting | bytes 14745600 | tf_op args[2]
  11.5 83.7 %late_interaction.1 = (f32[1,8]{1,0:T(1,128)}, f32[1,1]{1,0:T(1,128)}) custom-call(bf16[8,32,768]{2,1,0:T(8,128)(2,1)} %qh_hbm.1, bf16[8,300,768]{2,1,0:T(8,128)(2,1)} %copy.11.dh_hbm, bf16[8,2,300,768]{3,2,1,0:T(8,128)(2,1)} %copy.12.nh_hbm, bf16[768,128]{1,0:T(8,128)(2,1)} %w_ref.1, s32[8,32]{1,0:T(8,128)} %qmask_ref.1, s32[8,300]{1,0:T(8,128)} %dmask_ref.1, ...), custom_call_target="tpu_custom_call" | custom-call | tf_op jit(solution)/shard_map/late_interaction/pallas_call | solution.py:296
  95.2 1.2 %copy.17 = f32[8]{0:T(128)} copy(f32[8]{0:T(128)} %bitcast.4) | data formatting | bytes 64
Async XLA Ops:
  2.6 4.9 %copy-start = (bf16[8,2,300,768]{3,1,2,0:T(2,128)(2,1)S(1)}, bf16[8,2,300,768]{3,1,2,0:T(2,128)(2,1)}, u32[]{:S(2)}) copy-start(bf16[8,2,300,768]{3,1,2,0:T(2,128)(2,1)} %param.11) | copy-start | bytes 22118404
